TPU v7x, 32 devices: a whole 2x2x4 slice. The times are simulated.
32 devices in a mesh: grp: 2 (over core), dom: 16 (over z, y, x).
Axes of the slice: x: 2, y: 2, z: 4, core: 2. Of those that a mesh axis runs over, the one named last changes fastest.
Arguments:
- node_latent: bfloat16 [32768, 128], P(('grp', 'dom')), may hold values from -6 to 6
- edge_latent: bfloat16 [196608, 128], P(('grp', 'dom')), may hold values from -6 to 6
- mig_send: int32 [32, 256], P(('grp', 'dom')), may hold values from 0 to 1024, as said below
- mig_recv: int32 [32768], P(('grp', 'dom')), may hold values from 0 to 1279, as said below
- halo_send: int32 [32, 128], P(('grp', 'dom')), may hold values from 0 to 1024, as said below
- cross_send: int32 [32, 32], P(('grp', 'dom')), may hold values from 0 to 1024, as said below
- senders: int32 [196608], P(('grp', 'dom')), may hold values from 0 to 1183, as said below
- receivers: int32 [196608], P(('grp', 'dom')), may hold values from 0 to 1023
- edge_live: int32 [196608], P(('grp', 'dom')), may hold values from 0 to 1, as said below
- edge_w1: bfloat16 [384, 128], replicated, may hold values from -0.3125 to 0.3125
- edge_b1: float32 [128], replicated, may hold values from -2 to 2
- edge_w2: bfloat16 [128, 128], replicated, may hold values from -0.5 to 0.5
- edge_b2: float32 [128], replicated, may hold values from -2 to 2
- edge_gain: float32 [128], replicated, may hold values from 0.25 to 1.75
- edge_bias: float32 [128], replicated, may hold values from -2 to 2
- node_w1: bfloat16 [256, 128], replicated, may hold values from -0.375 to 0.375
- node_b1: float32 [128], replicated, may hold values from -2 to 2
- node_w2: bfloat16 [128, 128], replicated, may hold values from -0.5 to 0.5
- node_b2: float32 [128], replicated, may hold values from -2 to 2
- node_gain: float32 [128], replicated, may hold values from 0.25 to 1.75
- node_bias: float32 [128], replicated, may hold values from -2 to 2
Outputs:
- node_out: bfloat16 [32768, 128], P(('grp', 'dom'))
- edge_out: bfloat16 [196608, 128], P(('grp', 'dom'))
Inputs may be any that keep to these rules, and one draw needn't show every extreme that they name: `mig_send`: per partition, slot k * 64 + c names an old local row moving to the partition at distance o_k, or 1024 for an empty slot; live slots of one distance come first, every old row is named at most once, and a partition sends to a partition exactly as many rows as it receives from it. Where the peer exists, 32 or more slots of a distance are live; slots toward missing partitions are empty; in every draw some partition of each region fills all its slots both ways. `mig_recv`: for each partition, 1024 distinct entries of its source table: old rows it did not send and live arrived slots, each exactly once. `halo_send`: slot k * 32 + c names a new local row sent to the partition at distance o_k, or 1024 if empty; live slots come first, rows are distinct within a partition; where the peer exists 32 // 2 or more are live, and some partition of each region fills all slots whose peer exists. `cross_send`: new local rows sent to the same partition of the other region, or 1024 if empty; live slots come first, 16 or more live, distinct from that partition's halo_send rows; some partition of each region fills all. `senders`: each entry names a new local row (below 1024) or a live halo or cross slot of the extended table. `edge_live`: within a partition, the live edge slots are a prefix of at least 3072 slots; some partition is fully live in every draw.
All inputs are finite; a program needn't handle non-finite values.
Results may differ from a plain program's by a relative error of at most 0.0075.
Values may be sent and summed in bfloat16 or wider, within the bound.
No kernel may reach another device: no remote copies, remote signals or barrier semaphores. Data moves between devices by JAX's collectives and lax.ppermute only.
A program may use at most 64 MiB of HBM per device.

v0:
```python
import functools

import jax
import jax.numpy as jnp
from jax import lax
from jax.experimental import pallas as pl
from jax.experimental.pallas import tpu as pltpu
from jax.sharding import PartitionSpec as P


LANES = 128
EDGE_BLOCK = 1024
ANY = pl.BlockSpec(memory_space=pl.ANY)
EPSILON = 1e-05
BF16 = jnp.bfloat16
F32 = jnp.float32


def dot(a, b):
    return jnp.dot(a, b, preferred_element_type=F32)


def swapped(value, axis, partner_of):
    count = lax.axis_size(axis)
    pairs = []
    for i in range(count):
        j = partner_of(i)
        pairs.append((i, j if 0 <= j < count else i ^ 1))
    return lax.ppermute(value, axis, pairs)


def lane_ids(tile, shift):
    ids = lax.broadcasted_iota(jnp.int32, (LANES, LANES), 1) + (tile * LANES - shift)
    return ids.astype(F32).astype(BF16)


def spread(columns, b):
    return jnp.broadcast_to(columns[:, b : b + 1], (columns.shape[0], LANES))


def marks_from(values, count, shift):
    one, zero = jnp.ones((), BF16), jnp.zeros((), BF16)
    rows = values.shape[0]
    return jnp.concatenate(
        [jnp.where(values == lane_ids(t, shift)[:rows], one, zero) for t in range(count)], axis=1
    )


def split_index(rows, half):
    high = (rows >= half).astype(F32)
    low = rows.astype(F32) - high * half - half // 2
    return low.T.astype(BF16), high.T


def lookup(low, high, b, table2):
    half = table2.shape[0]
    both = dot(marks_from(spread(low, b), half // LANES, half // 2), table2)
    return jnp.where(spread(high, b) > 0.5, both[:, LANES:], both[:, :LANES])


def side_by_side(table):
    half = table.shape[0] // 2
    return jnp.concatenate([table[:half], table[half:]], axis=1)


def twice(w):
    zero = jnp.zeros_like(w)
    return jnp.concatenate(
        [jnp.concatenate([w, zero], axis=1), jnp.concatenate([zero, w], axis=1)], axis=0
    )


def eight(row):
    return jnp.broadcast_to(row, (8, row.shape[1]))


def first_kernel(out_ref):
    out_ref[...] = jnp.zeros_like(out_ref)


def leave_kernel(node_ref, send_ref, _, near_ref, far_ref):
    table = side_by_side(node_ref[...])
    pieces = []
    for b in range(send_ref.shape[1] // LANES):
        low, high = split_index(eight(send_ref[:, b * LANES : (b + 1) * LANES]), table.shape[0])
        pieces.append(lookup(low, high, 0, table))
    rows = jnp.concatenate(pieces, axis=0).astype(BF16)
    quarter = rows.shape[0] // 4
    near_ref[...] = rows[quarter : 3 * quarter]
    far_ref[...] = jnp.concatenate([rows[:quarter], rows[3 * quarter :]], axis=0)


def own_kernel(
    edge_ref, w1_ref, b1_ref, send_ref, recv_ref, live_ref, mig_ref, halo_ref, cross_ref, _,
    own_ref, w1_copy, send_copy, recv_copy, live_copy, mig_copy, halo_copy, cross_copy,
):
    w1_copy[...] = w1_ref[...]
    send_copy[...] = send_ref[...]
    recv_copy[...] = recv_ref[...]
    live_copy[...] = live_ref[...]
    mig_copy[...] = mig_ref[...]
    halo_copy[...] = halo_ref[...]
    cross_copy[...] = cross_ref[...]
    wa = twice(w1_ref[:LANES, :])
    b1 = b1_ref[...]
    half = EDGE_BLOCK // 2

    def step(i, carry):
        at = pl.multiple_of(i * EDGE_BLOCK, EDGE_BLOCK)
        top, bottom = edge_ref[pl.ds(at, half), :], edge_ref[pl.ds(at + half, half), :]
        pair = dot(jnp.concatenate([top, bottom], axis=1), wa)
        own_ref[pl.ds(at, half), :] = pair[:, :LANES] + b1
        own_ref[pl.ds(at + half, half), :] = pair[:, LANES:] + b1
        return carry

    lax.fori_loop(0, edge_ref.shape[0] // EDGE_BLOCK, step, 0)


def target_kernel(recv_ref, _, marks_ref):
    half = marks_ref.shape[0]
    one, zero = jnp.ones((), BF16), jnp.zeros((), BF16)
    ids = (lax.broadcasted_iota(jnp.int32, (half, LANES), 0) - half // 2).astype(F32).astype(BF16)
    recv = recv_ref[...]
    low = jnp.where(recv >= half, recv - half, recv) - half // 2
    low = low.astype(F32)
    for b in range(recv.shape[0]):
        row = jnp.broadcast_to(low[b : b + 1, :], (16, LANES)).astype(BF16)
        row = jnp.concatenate([row] * (half // 16), axis=0)
        marks_ref[:, b * LANES : (b + 1) * LANES] = jnp.where(ids == row, one, zero)


def fresh_kernel(
    node_ref, arrived_ref, recv_ref, halo_ref, cross_ref, fresh_ref, near_ref, far_ref, cross_out
):
    table = side_by_side(node_ref[...])
    n = 2 * table.shape[0]
    recv = recv_ref[...]
    low, high = split_index(recv, table.shape[0])
    moved = (recv - n).astype(F32).T.astype(BF16)
    arrived = arrived_ref[...]
    pieces = []
    for b in range(n // LANES):
        marks = marks_from(spread(moved, b), arrived.shape[0] // LANES, 0)
        pieces.append((lookup(low, high, b, table) + dot(marks, arrived)).astype(BF16))
    fresh = jnp.concatenate(pieces, axis=0)
    fresh_ref[...] = fresh
    table = side_by_side(fresh)
    low, high = split_index(eight(halo_ref[...]), table.shape[0])
    halo = lookup(low, high, 0, table).astype(BF16)
    quarter = halo.shape[0] // 4
    near_ref[...] = halo[quarter : 3 * quarter]
    far_ref[...] = jnp.concatenate([halo[:quarter], halo[3 * quarter :]], axis=0)
    low, high = split_index(eight(cross_ref[...]), table.shape[0])
    cross_out[...] = lookup(low, high, 0, table).astype(BF16)


def pre_kernel(before_ref, fresh_ref, index_ref, w_ref, _, out_ref, *, part):
    table = side_by_side(dot(fresh_ref[...], w_ref[part * LANES : (part + 1) * LANES, :]).astype(BF16))
    for i in range(out_ref.shape[0] // EDGE_BLOCK):
        low, high = split_index(index_ref[i * 8 : (i + 1) * 8, :], table.shape[0])
        for b in range(EDGE_BLOCK // LANES):
            at = slice(i * EDGE_BLOCK + b * LANES, i * EDGE_BLOCK + (b + 1) * LANES)
            out_ref[at, :] = before_ref[at, :] + lookup(low, high, b, table)


def edge_kernel(
    pre_ref, edge_ref, fresh_ref, halo_ref, cross_ref, send_ref, recv_ref, live_ref, target_ref,
    w1_ref, w2_ref, b2_ref, gain_ref, bias_ref,
    nw1_ref, nb1_ref, nw2_ref, nb2_ref, ngain_ref, nbias_ref,
    node_out_ref, edge_out_ref,
    new_ref, acc_ref, hidden_ref, packed_ref, node_ref, sems, node_sems,
):
    n = fresh_ref.shape[0]
    nodes_half = n // 2
    block = EDGE_BLOCK
    quarters = block // (2 * LANES)

    r = lax.broadcasted_iota(jnp.int32, (2 * LANES, 2 * LANES), 0) // LANES
    c = lax.broadcasted_iota(jnp.int32, (2 * LANES, 2 * LANES), 1) // LANES
    averages = jnp.where(r == c, 1.0 / LANES, 0.0).astype(BF16)
    b2 = b2_ref[...]
    b2 = b2 - jnp.mean(b2, axis=-1, keepdims=True)
    b2 = jnp.concatenate([b2, b2], axis=1)
    remote_rows = jnp.concatenate([halo_ref[...], cross_ref[...]], axis=0)
    tx = dot(remote_rows, w1_ref[LANES : 2 * LANES, :]).astype(BF16)
    tx = jnp.concatenate([tx, jnp.zeros((2 * LANES - tx.shape[0], LANES), BF16)], axis=0)
    w2 = w2_ref[...].astype(F32)
    w2 = twice((w2 - jnp.mean(w2, axis=-1, keepdims=True)).astype(BF16))
    gain, bias = gain_ref[...], bias_ref[...]
    acc_ref[...] = jnp.zeros_like(acc_ref)

    def rows_of(j, offset, size):
        return pl.ds(pl.multiple_of(j * block + offset, LANES), size)

    def tile_of(ref, j):
        return ref[pl.ds(pl.multiple_of(j * 8, 8), 8), :]

    def copy_out(j):
        at = rows_of(j, 0, block)
        return pltpu.make_async_copy(new_ref.at[at, :], edge_out_ref.at[at, :], sems.at[j])

    def look(remote, b):
        marks = [marks_from(spread(remote, 2 * b + k), 2, 0) for k in range(2)]
        return dot(jnp.concatenate(marks, axis=0), tx)

    def hide(j, b, found):
        pre = pre_ref[rows_of(j, 2 * b * LANES, 2 * LANES), :] + found
        hidden_ref[2 * b * LANES : 2 * (b + 1) * LANES, :] = jnp.maximum(pre, 0.0).astype(BF16)

    def second(b):
        at = 2 * b * LANES
        top, bottom = hidden_ref[at : at + LANES, :], hidden_ref[at + LANES : at + 2 * LANES, :]
        return dot(jnp.concatenate([top, bottom], axis=1), w2) + b2

    def gather_part(j, b):
        at = slice(2 * b * LANES, 2 * (b + 1) * LANES)
        return dot(target_ref[:, rows_of(j, at.start, 2 * LANES)], packed_ref[at, :])

    def finish(j, b, centre, spreads, live, high):
        normed = centre * lax.rsqrt(spreads + EPSILON)
        for k in range(2):
            place = 2 * b + k
            at = rows_of(j, place * LANES, LANES)
            message = normed[:, k * LANES : (k + 1) * LANES] * gain + bias
            kept = message.astype(BF16) * spread(live, place)
            new_ref[at, :] = edge_ref[at, :] + kept
            upper = kept * spread(high, place)
            local = slice(place * LANES, (place + 1) * LANES)
            packed_ref[local, :LANES] = kept - upper
            packed_ref[local, LANES:] = upper

    def round_of(j, ahead, behind):
        live = tile_of(live_ref, j).astype(F32).T.astype(BF16)
        high = (tile_of(recv_ref, j) >= nodes_half).astype(F32).T.astype(BF16)
        if ahead:
            remote = (tile_of(send_ref, j + 1) - n).astype(F32).T.astype(BF16)
        centres, total, waiting = {}, None, []
        for b in range(quarters + 1):
            if b < quarters:
                centres[b] = second(b)
                if ahead:
                    found = look(remote, b)
            if b > 0:
                p = b - 1
                if behind:
                    part = gather_part(j - 1, p)
                    total = part if total is None else total + part
                spreads = dot((centres[p] * centres[p]).astype(BF16), averages)
                waiting.append((p, spreads))
            if b < quarters and ahead:
                hide(j + 1, b, found)
            if len(waiting) > 1 or b == quarters:
                for p, spreads in waiting[: len(waiting) if b == quarters else 1]:
                    finish(j, p, centres[p], spreads, live, high)
                waiting = waiting[1:]
        copy_out(j).start()
        if behind:
            acc_ref[...] += total

    steps = pre_ref.shape[0] // block
    remote = (tile_of(send_ref, 0) - n).astype(F32).T.astype(BF16)
    for b in range(quarters):
        hide(0, b, look(remote, b))
    round_of(0, True, False)

    for j in range(1, steps - 1):
        round_of(j, True, True)
    round_of(steps - 1, False, True)
    acc_ref[...] += dot(target_ref[:, rows_of(steps - 1, 0, block)], packed_ref[...])

    nb2 = nb2_ref[...]
    nb2 = nb2 - jnp.mean(nb2, axis=-1, keepdims=True)
    nb2 = jnp.concatenate([nb2, nb2], axis=1)
    nw2 = nw2_ref[...].astype(F32)
    nw2 = twice((nw2 - jnp.mean(nw2, axis=-1, keepdims=True)).astype(BF16))
    nw1, nb1 = nw1_ref[...], nb1_ref[...]
    parts = 4
    size = nodes_half // parts
    mine = lambda p, k: slice(k * nodes_half + p * size, k * nodes_half + (p + 1) * size)
    hidden = []
    for p in range(parts):
        both = []
        for k in range(2):
            inbound = acc_ref[p * size : (p + 1) * size, k * LANES : (k + 1) * LANES].astype(BF16)
            first = dot(jnp.concatenate([fresh_ref[mine(p, k), :], inbound], axis=1), nw1)
            both.append(jnp.maximum(first + nb1, 0.0).astype(BF16))
        hidden.append(jnp.concatenate(both, axis=1))
    centres = [dot(h, nw2) + nb2 for h in hidden]
    spreads = [dot((centre * centre).astype(BF16), averages) for centre in centres]
    node_copies = []
    for p in range(parts):
        normed = centres[p] * lax.rsqrt(spreads[p] + EPSILON)
        for k in range(2):
            update = normed[:, k * LANES : (k + 1) * LANES] * ngain_ref[...] + nbias_ref[...]
            at = mine(p, k)
            node_ref[at, :] = (fresh_ref[at, :].astype(F32) + update).astype(BF16)
            copy = pltpu.make_async_copy(
                node_ref.at[at, :], node_out_ref.at[at, :], node_sems.at[2 * p + k]
            )
            copy.start()
            node_copies.append(copy)
    for j in range(steps):
        copy_out(j).wait()
    for copy in node_copies:
        copy.wait()


def outward(near_partner, far, d):
    rows = far.shape[0] // 2
    even_pair = (d // 2) % 2 == 0
    plus = jnp.concatenate([far[rows:], near_partner[rows:]], axis=0)
    minus = jnp.concatenate([far[:rows], near_partner[:rows]], axis=0)
    outer = swapped(
        jnp.where(even_pair, minus, plus), "dom", lambda i: i - 2 if i % 4 < 2 else i + 2
    )
    inner = swapped(
        jnp.where(even_pair, plus, minus), "dom", lambda i: i + 2 if i % 4 < 2 else i - 2
    )
    return outer, inner


def inward(near_partner, outer, inner, d):
    rows = near_partner.shape[0] // 2
    odd = d % 2 == 1
    even_pair = (d // 2) % 2 == 0
    before = jnp.where(even_pair, outer, inner)
    after = jnp.where(even_pair, inner, outer)
    return jnp.concatenate(
        [
            after[:rows],
            jnp.where(odd, after[rows:], near_partner[:rows]),
            jnp.where(odd, near_partner[rows:], before[rows:]),
            before[:rows],
        ],
        axis=0,
    )


def call(kernel, out_shape, limit, flops=10**9, **kw):
    return pl.pallas_call(
        kernel,
        out_shape=out_shape,
        compiler_params=pltpu.CompilerParams(vmem_limit_bytes=limit << 20),
        cost_estimate=pl.CostEstimate(flops=flops, bytes_accessed=10**6, transcendentals=0),
        **kw,
    )


VM = pl.BlockSpec(memory_space=pltpu.VMEM)


def like(*arrays):
    return [jax.ShapeDtypeStruct(a.shape, a.dtype) for a in arrays]


def body(
    node_latent, edge_latent, mig_send, mig_recv, halo_send, cross_send, senders, receivers, edge_live,
    edge_w1, edge_b1, edge_w2, edge_b2, edge_gain, edge_bias,
    node_w1, node_b1, node_w2, node_b2, node_gain, node_bias,
):
    n, latent = node_latent.shape
    edges = edge_latent.shape[0]
    d = lax.axis_index("dom")
    move = mig_send.shape[1]
    halo = halo_send.shape[1]
    cross = cross_send.shape[1]
    shape = jax.ShapeDtypeStruct
    row = lambda v: v.reshape(1, latent)
    tiles = lambda v: v.reshape(-1, LANES)

    (first,) = call(first_kernel, [shape((8, LANES), F32)], 1)()
    near, far = call(
        leave_kernel, [shape((move // 2, latent), BF16)] * 2, 4, in_specs=[VM, VM, ANY]
    )(node_latent, mig_send, first)
    partner = swapped(near, "dom", lambda i: i ^ 1)
    args = (
        edge_latent, edge_w1, row(edge_b1), tiles(senders), tiles(receivers), tiles(edge_live),
        tiles(mig_recv), halo_send, cross_send,
    )
    own, w1, send, recv, live, mig, halo_index, cross_index = call(
        own_kernel,
        [shape((edges, latent), F32)] + like(args[1], *args[3:]),
        10,
        in_specs=[VM] * 9 + [ANY],
    )(*args, near)
    partner, own, recv = lax.optimization_barrier((partner, own, recv))
    outer, inner = outward(partner, far, d)
    (targets,) = call(
        target_kernel, [shape((n // 2, edges), BF16)], 10, in_specs=[VM, ANY]
    )(recv, partner)
    outer, inner, targets = lax.optimization_barrier((outer, inner, targets))
    arrived = inward(partner, outer, inner, d)

    fresh, near, far, cross_out = call(
        fresh_kernel,
        [shape((n, latent), BF16)] + [shape((halo // 2, latent), BF16)] * 2 + [shape((cross, latent), BF16)],
        8,
    )(node_latent, arrived, mig, halo_index, cross_index)
    partner = swapped(near, "dom", lambda i: i ^ 1)
    cross_in = lax.ppermute(cross_out, "grp", [(i, i ^ 1) for i in range(lax.axis_size("grp"))])
    (pre,) = call(
        functools.partial(pre_kernel, part=2), [shape((edges, latent), F32)], 10,
        in_specs=[VM] * 4 + [ANY],
    )(own, fresh, recv, w1, near)
    partner, pre = lax.optimization_barrier((partner, pre))
    outer, inner = outward(partner, far, d)
    (pre,) = call(
        functools.partial(pre_kernel, part=1), [shape((edges, latent), F32)], 10,
        in_specs=[VM] * 4 + [ANY],
    )(pre, fresh, send, w1, partner)
    outer, inner, cross_in, pre = lax.optimization_barrier((outer, inner, cross_in, pre))
    halo_in = inward(partner, outer, inner, d)
    node_out, edge_out = call(
        edge_kernel,
        [shape((n, latent), BF16), shape((edges, latent), BF16)],
        16,
        flops=10**10,
        out_specs=[ANY, ANY],
        scratch_shapes=[
            pltpu.VMEM((edges, latent), BF16),
            pltpu.VMEM((n // 2, 2 * latent), F32),
            pltpu.VMEM((EDGE_BLOCK, latent), BF16),
            pltpu.VMEM((EDGE_BLOCK, 2 * latent), BF16),
            pltpu.VMEM((n, latent), BF16),
            pltpu.SemaphoreType.DMA((edges // EDGE_BLOCK,)),
            pltpu.SemaphoreType.DMA((8,)),
        ],
    )(
        pre, edge_latent, fresh, halo_in, cross_in, send, recv, live, targets,
        w1, edge_w2, row(edge_b2), row(edge_gain), row(edge_bias),
        node_w1, row(node_b1), node_w2, row(node_b2), row(node_gain), row(node_bias),
    )
    return node_out, edge_out


def solution(mesh):
    split, split1, copied = P(("grp", "dom"), None), P(("grp", "dom")), P()
    placed = (
        split, split, split, split1, split, split, split1, split1, split1,
    ) + (copied,) * 12
    return jax.shard_map(
        body, mesh=mesh, in_specs=placed, out_specs=(split, split), check_vma=False
    )
```

profile of v0, /device:TPU:0, one launch (start us, length us, event | category | flops | bytes accessed | tf_op | source)
XLA Modules:
  0.0 29.9 jit_solution(5583424479074759369)
XLA Ops:
  0.6 0.0 copy-start.2
  0.7 0.0 copy-start
  0.8 0.8 %copy-done.2 = bf16[1024,128]{1,0:T(8,128)(2,1)S(1)} copy-done((bf16[1024,128]{1,0:T(8,128)(2,1)S(1)}, bf16[1024,128]{1,0:T(8,128)(2,1)}, u32[]{:S(2)}) %copy-start.2) | copy-done | bytes 262168
  1.6 0.3 %shard_map.213 = (bf16[128,128]{1,0:T(8,128)(2,1)S(1)}, bf16[128,128]{1,0:T(8,128)(2,1)S(1)}) custom-call(bf16[1024,128]{1,0:T(8,128)(2,1)S(1)} %copy-done.2, s32[1,256]{1,0:T(1,128)S(1)} %copy-done.12, f32[8,128]{1,0:T(8,128)S(1)} %shard_map.212._), custom_call_target="tpu_custom_call" | custom-call | flops 1000000000 | bytes 1000000 | tf_op jit(solution)/shard_map/pallas_call | solution.py:372
  1.9 3.0 %collective-permute-start = (bf16[128,128]{1,0:T(8,128)(2,1)S(1)}, bf16[128,128]{1,0:T(8,128)(2,1)S(1)}, u32[]{:S(2)}, u32[]{:S(2)}) collective-permute-start(bf16[128,128]{1,0:T(8,128)(2,1)S(1)} %get-tuple-element.29._), channel_id=1, source_target_pairs={{0,1},{1,0},{2,3},{3,2},{4,5},{5,4},{6,7},{7,6},{8,9},{9,8},{10,11... | collective-permute-start | bytes 98312 | tf_op jit(solution)/shard_map/ppermute | solution.py:29
  5.1 1.4 %shard_map.214 = (f32[6144,128]{1,0:T(8,128)S(1)}, bf16[384,128]{1,0:T(8,128)(2,1)S(1)}, s32[48,128]{1,0:T(8,128)S(1)}, s32[48,128]{1,0:T(8,128)S(1)}, s32[48,12...) custom-call(bf16[6144,128]{1,0:T(8,128)(2,1)S(1)} %copy-done, ...), custom_call_target="tpu_custom_call" | custom-call | flops 1000000000 | bytes 1000000 | tf_op jit(solution)/shard_map/pallas_call | solution.py:380
  6.5 0.4 %collective-permute-done._ = bf16[128,128]{1,0:T(8,128)(2,1)S(1)} collective-permute-done((bf16[128,128]{1,0:T(8,128)(2,1)S(1)}, bf16[128,128]{1,0:T(8,128)(2,1)S(1)}, u32[]{:S(2)}, u32[]{:S(2)}) %collective-permute-start) | collective-permute-done | bytes 32800 | tf_op jit(solution)/shard_map/ppermute | solution.py:29
  6.9 2.1 %collective-permute-start.2 = (bf16[128,128]{1,0:T(8,128)(2,1)S(1)}, bf16[128,128]{1,0:T(8,128)(2,1)S(1)}, u32[]{:S(2)}, u32[]{:S(2)}) collective-permute-start(bf16[128,128]{1,0:T(8,128)(2,1)S(1)} %get-tuple-element.56), channel_id=1, source_target_pairs={{0,2},{1,3},{2,0},{3,1},{4,6},{5,7},{6,4},{7,5},{8,10},{9,11},{10,... | collective-permute-start | bytes 98312 | tf_op jit(solution)/shard_map/ppermute | solution.py:29
  9.0 1.5 %collective-permute-start.1 = (bf16[128,128]{1,0:T(8,128)(2,1)S(1)}, bf16[128,128]{1,0:T(8,128)(2,1)S(1)}, u32[]{:S(2)}, u32[]{:S(2)}) collective-permute-start(bf16[128,128]{1,0:T(8,128)(2,1)S(1)} %get-tuple-element.57), channel_id=1, source_target_pairs={{0,1},{1,0},{2,4},{3,5},{4,2},{5,3},{6,8},{7,9},{8,6},{9,7},{10,12... | collective-permute-start | bytes 98312 | tf_op jit(solution)/shard_map/ppermute | solution.py:29
  10.5 1.6 %shard_map.215.target_ref = bf16[512,6144]{1,0:T(8,128)(2,1)S(1)} custom-call(s32[48,128]{1,0:T(8,128)S(1)} %get-tuple-element.33.recv_ref.index_ref, bf16[128,128]{1,0:T(8,128)(2,1)S(1)} %collective-permute-done._), custom_call_target="tpu_custom_call" | custom-call | flops 1000000000 | bytes 1000000 | tf_op jit(solution)/shard_map/pallas_call | solution.py:388
  12.1 0.8 %collective-permute-done.1 = bf16[128,128]{1,0:T(8,128)(2,1)S(1)} collective-permute-done((bf16[128,128]{1,0:T(8,128)(2,1)S(1)}, bf16[128,128]{1,0:T(8,128)(2,1)S(1)}, u32[]{:S(2)}, u32[]{:S(2)}) %collective-permute-start.1) | collective-permute-done | bytes 32800 | tf_op jit(solution)/shard_map/ppermute | solution.py:29
  13.0 1.0 %shard_map.216 = (bf16[1024,128]{1,0:T(8,128)(2,1)S(1)}, bf16[64,128]{1,0:T(8,128)(2,1)S(1)}, bf16[64,128]{1,0:T(8,128)(2,1)S(1)}, bf16[32,128]{1,0:T(8,128)(2,1)S(1)}) custom-call(bf16[1024,128]{1,0:T(8,128)(2,1)S(1)} %copy-done.3, bf16[256,128]{1,0:T(8,128)(2,1)S(1)} %pad_maximum_fusion.arrived_ref, s32[8,128]{1,0:T(8,128)S(1)} %get-tuple-element.36.recv_ref, ...), custom_call_target="tpu_custom_call" | custom-call | flops 1000000000 | bytes 1000000 | tf_op jit(solution)/shard_map/pallas_call | solution.py:394
  14.0 0.1 collective-permute-start.6
  14.1 1.6 %collective-permute-start.3 = (bf16[64,128]{1,0:T(8,128)(2,1)S(1)}, bf16[64,128]{1,0:T(8,128)(2,1)S(1)}, u32[]{:S(2)}, u32[]{:S(2)}) collective-permute-start(bf16[64,128]{1,0:T(8,128)(2,1)S(1)} %get-tuple-element.40._), channel_id=1, source_target_pairs={{0,1},{1,0},{2,3},{3,2},{4,5},{5,4},{6,7},{7,6},{8,9},{9,8},{10,11... | collective-permute-start | bytes 49160 | tf_op jit(solution)/shard_map/ppermute | solution.py:29
  15.7 2.2 %shard_map.217.before_ref = f32[6144,128]{1,0:T(8,128)S(1)} custom-call(f32[6144,128]{1,0:T(8,128)S(1)} %get-tuple-element.41.before_ref, bf16[1024,128]{1,0:T(8,128)(2,1)S(1)} %get-tuple-element.42.fresh_ref, s32[48,128]{1,0:T(8,128)S(1)} %get-tuple-element.33.recv_ref.index_ref, bf16[384,128]{1,0:T(8,128)(2,1)S(1)} %get-tuple-element.43.w_ref.w1_ref, ...), custom_call_target="tpu_custom_call" | custom-call | flops 1000000000 | bytes 1000000 | tf_op jit(solution)/shard_map/pallas_call | solution.py:401
  17.9 0.0 collective-permute-done.3._
  17.9 1.5 %collective-permute-start.5 = (bf16[64,128]{1,0:T(8,128)(2,1)S(1)}, bf16[64,128]{1,0:T(8,128)(2,1)S(1)}, u32[]{:S(2)}, u32[]{:S(2)}) collective-permute-start(bf16[64,128]{1,0:T(8,128)(2,1)S(1)} %get-tuple-element.60), channel_id=1, source_target_pairs={{0,2},{1,3},{2,0},{3,1},{4,6},{5,7},{6,4},{7,5},{8,10},{9,11},{10,... | collective-permute-start | bytes 49160 | tf_op jit(solution)/shard_map/ppermute | solution.py:29
  19.4 1.5 %collective-permute-start.4 = (bf16[64,128]{1,0:T(8,128)(2,1)S(1)}, bf16[64,128]{1,0:T(8,128)(2,1)S(1)}, u32[]{:S(2)}, u32[]{:S(2)}) collective-permute-start(bf16[64,128]{1,0:T(8,128)(2,1)S(1)} %get-tuple-element.61), channel_id=1, source_target_pairs={{0,1},{1,0},{2,4},{3,5},{4,2},{5,3},{6,8},{7,9},{8,6},{9,7},{10,12... | collective-permute-start | bytes 49160 | tf_op jit(solution)/shard_map/ppermute | solution.py:29
  20.9 0.0 copy-start.16
  20.9 0.0 copy-start.18
  20.9 0.0 copy-start.19
  21.0 0.0 copy-start.22
  21.0 2.3 %shard_map.218.pre_ref = f32[6144,128]{1,0:T(8,128)S(1)} custom-call(f32[6144,128]{1,0:T(8,128)S(1)} %shard_map.217.before_ref, bf16[1024,128]{1,0:T(8,128)(2,1)S(1)} %get-tuple-element.42.fresh_ref, s32[48,128]{1,0:T(8,128)S(1)} %get-tuple-element.47.index_ref.send_ref, bf16[384,128]{1,0:T(8,128)(2,1)S(1)} %get-tuple-element.43.w_ref.w1_ref, ...), custom_call_target="tpu_custom_call" | custom-call | flops 1000000000 | bytes 1000000 | tf_op jit(solution)/shard_map/pallas_call | solution.py:407
  23.4 6.5 %shard_map.219 = (bf16[1024,128]{1,0:T(8,128)(2,1)}, bf16[6144,128]{1,0:T(8,128)(2,1)}) custom-call(f32[6144,128]{1,0:T(8,128)S(1)} %shard_map.218.pre_ref, bf16[6144,128]{1,0:T(8,128)(2,1)S(1)} %copy-done.1, bf16[1024,128]{1,0:T(8,128)(2,1)S(1)} %get-tuple-element.42.fresh_ref, bf16[128,128]{1,0:T(8,128)(2,1)S(1)} %pad_maximum_fusion.3.halo_ref, ...), custom_call_target="tpu_custom_call" | custom-call | flops 10000000000 | bytes 1000000 | tf_op jit(solution)/shard_map/pallas_call | solution.py:413
  (56 shorter events, 0.2 us)
Async XLA Ops:
  0.7 4.3 %copy-start = (bf16[6144,128]{1,0:T(8,128)(2,1)S(1)}, bf16[6144,128]{1,0:T(8,128)(2,1)}, u32[]{:S(2)}) copy-start(bf16[6144,128]{1,0:T(8,128)(2,1)} %edge_ref.3) | copy-start | bytes 4718596
  0.7 4.3 %copy-start.13 = (f32[128]{0:T(128)S(1)}, f32[128]{0:T(128)}, u32[]{:S(2)}) copy-start(f32[128]{0:T(128)} %param.31) | copy-start | bytes 1540
  0.7 4.3 %copy-start.4 = (bf16[384,128]{1,0:T(8,128)(2,1)S(1)}, bf16[384,128]{1,0:T(8,128)(2,1)}, u32[]{:S(2)}) copy-start(bf16[384,128]{1,0:T(8,128)(2,1)} %w1_ref.1) | copy-start | bytes 294916
  0.7 4.3 %copy-start.10 = (s32[6144]{0:T(1024)S(1)}, s32[6144]{0:T(1024)}, u32[]{:S(2)}) copy-start(s32[6144]{0:T(1024)} %param.29) | copy-start | bytes 73732
  0.7 4.3 %copy-start.9 = (s32[6144]{0:T(1024)S(1)}, s32[6144]{0:T(1024)}, u32[]{:S(2)}) copy-start(s32[6144]{0:T(1024)} %param.28) | copy-start | bytes 73732
  0.7 4.3 %copy-start.8 = (s32[6144]{0:T(1024)S(1)}, s32[6144]{0:T(1024)}, u32[]{:S(2)}) copy-start(s32[6144]{0:T(1024)} %param.27) | copy-start | bytes 73732
  0.7 4.3 %copy-start.15 = (s32[1,32]{1,0:T(1,128)S(1)}, s32[1,32]{1,0:T(1,128)}, u32[]{:S(2)}) copy-start(s32[1,32]{1,0:T(1,128)} %cross_ref.1) | copy-start | bytes 388
  0.7 4.3 %copy-start.14 = (s32[1,128]{1,0:T(1,128)S(1)}, s32[1,128]{1,0:T(1,128)}, u32[]{:S(2)}) copy-start(s32[1,128]{1,0:T(1,128)} %halo_ref.1) | copy-start | bytes 1540
  0.7 4.3 %copy-start.11 = (s32[1024]{0:T(1024)S(1)}, s32[1024]{0:T(1024)}, u32[]{:S(2)}) copy-start(s32[1024]{0:T(1024)} %param.24) | copy-start | bytes 12292
  1.9 4.9 %collective-permute-start = (bf16[128,128]{1,0:T(8,128)(2,1)S(1)}, bf16[128,128]{1,0:T(8,128)(2,1)S(1)}, u32[]{:S(2)}, u32[]{:S(2)}) collective-permute-start(bf16[128,128]{1,0:T(8,128)(2,1)S(1)} %get-tuple-element.29._), channel_id=1, source_target_pairs={{0,1},{1,0},{2,3},{3,2},{4,5},{5,4},{6,7},{7,6},{8,9},{9,8},{10,11... | collective-permute-start | bytes 98312 | tf_op jit(solution)/shard_map/ppermute | solution.py:29
  6.9 5.2 %collective-permute-start.2 = (bf16[128,128]{1,0:T(8,128)(2,1)S(1)}, bf16[128,128]{1,0:T(8,128)(2,1)S(1)}, u32[]{:S(2)}, u32[]{:S(2)}) collective-permute-start(bf16[128,128]{1,0:T(8,128)(2,1)S(1)} %get-tuple-element.56), channel_id=1, source_target_pairs={{0,2},{1,3},{2,0},{3,1},{4,6},{5,7},{6,4},{7,5},{8,10},{9,11},{10,... | collective-permute-start | bytes 98312 | tf_op jit(solution)/shard_map/ppermute | solution.py:29
  9.0 4.0 %copy-start.3 = (bf16[1024,128]{1,0:T(8,128)(2,1)S(1)}, bf16[1024,128]{1,0:T(8,128)(2,1)}, u32[]{:S(2)}) copy-start(bf16[1024,128]{1,0:T(8,128)(2,1)} %node_ref.3) | copy-start | bytes 786436
  9.0 3.9 %collective-permute-start.1 = (bf16[128,128]{1,0:T(8,128)(2,1)S(1)}, bf16[128,128]{1,0:T(8,128)(2,1)S(1)}, u32[]{:S(2)}, u32[]{:S(2)}) collective-permute-start(bf16[128,128]{1,0:T(8,128)(2,1)S(1)} %get-tuple-element.57), channel_id=1, source_target_pairs={{0,1},{1,0},{2,4},{3,5},{4,2},{5,3},{6,8},{7,9},{8,6},{9,7},{10,12... | collective-permute-start | bytes 98312 | tf_op jit(solution)/shard_map/ppermute | solution.py:29
  14.0 9.2 %collective-permute-start.6 = (bf16[32,128]{1,0:T(8,128)(2,1)S(1)}, bf16[32,128]{1,0:T(8,128)(2,1)S(1)}, u32[]{:S(2)}, u32[]{:S(2)}) collective-permute-start(bf16[32,128]{1,0:T(8,128)(2,1)S(1)} %get-tuple-element.45), channel_id=1, source_target_pairs={{0,16},{16,0},{1,17},{17,1},{2,18},{18,2},{3,19},{19,3},{4,20},{20... | collective-permute-start | bytes 24584 | tf_op jit(solution)/shard_map/ppermute | solution.py:400
  14.1 3.8 %collective-permute-start.3 = (bf16[64,128]{1,0:T(8,128)(2,1)S(1)}, bf16[64,128]{1,0:T(8,128)(2,1)S(1)}, u32[]{:S(2)}, u32[]{:S(2)}) collective-permute-start(bf16[64,128]{1,0:T(8,128)(2,1)S(1)} %get-tuple-element.40._), channel_id=1, source_target_pairs={{0,1},{1,0},{2,3},{3,2},{4,5},{5,4},{6,7},{7,6},{8,9},{9,8},{10,11... | collective-permute-start | bytes 49160 | tf_op jit(solution)/shard_map/ppermute | solution.py:29
  17.9 5.3 %collective-permute-start.5 = (bf16[64,128]{1,0:T(8,128)(2,1)S(1)}, bf16[64,128]{1,0:T(8,128)(2,1)S(1)}, u32[]{:S(2)}, u32[]{:S(2)}) collective-permute-start(bf16[64,128]{1,0:T(8,128)(2,1)S(1)} %get-tuple-element.60), channel_id=1, source_target_pairs={{0,2},{1,3},{2,0},{3,1},{4,6},{5,7},{6,4},{7,5},{8,10},{9,11},{10,... | collective-permute-start | bytes 49160 | tf_op jit(solution)/shard_map/ppermute | solution.py:29
  19.4 3.9 %collective-permute-start.4 = (bf16[64,128]{1,0:T(8,128)(2,1)S(1)}, bf16[64,128]{1,0:T(8,128)(2,1)S(1)}, u32[]{:S(2)}, u32[]{:S(2)}) collective-permute-start(bf16[64,128]{1,0:T(8,128)(2,1)S(1)} %get-tuple-element.61), channel_id=1, source_target_pairs={{0,1},{1,0},{2,4},{3,5},{4,2},{5,3},{6,8},{7,9},{8,6},{9,7},{10,12... | collective-permute-start | bytes 49160 | tf_op jit(solution)/shard_map/ppermute | solution.py:29
  20.9 2.5 %copy-start.7 = (bf16[128,128]{1,0:T(8,128)(2,1)S(1)}, bf16[128,128]{1,0:T(8,128)(2,1)}, u32[]{:S(2)}) copy-start(bf16[128,128]{1,0:T(8,128)(2,1)} %nw2_ref.1) | copy-start | bytes 98308
  20.9 2.5 %copy-start.16 = (f32[128]{0:T(128)S(1)}, f32[128]{0:T(128)}, u32[]{:S(2)}) copy-start(f32[128]{0:T(128)} %param.33) | copy-start | bytes 1540
  20.9 2.5 %copy-start.17 = (f32[128]{0:T(128)S(1)}, f32[128]{0:T(128)}, u32[]{:S(2)}) copy-start(f32[128]{0:T(128)} %param.34) | copy-start | bytes 1540
  20.9 2.5 %copy-start.18 = (f32[128]{0:T(128)S(1)}, f32[128]{0:T(128)}, u32[]{:S(2)}) copy-start(f32[128]{0:T(128)} %param.35) | copy-start | bytes 1540
  20.9 2.5 %copy-start.19 = (f32[128]{0:T(128)S(1)}, f32[128]{0:T(128)}, u32[]{:S(2)}) copy-start(f32[128]{0:T(128)} %param.37) | copy-start | bytes 1540
  20.9 2.5 %copy-start.20 = (f32[128]{0:T(128)S(1)}, f32[128]{0:T(128)}, u32[]{:S(2)}) copy-start(f32[128]{0:T(128)} %param.39) | copy-start | bytes 1540
  21.0 2.5 %copy-start.21 = (f32[128]{0:T(128)S(1)}, f32[128]{0:T(128)}, u32[]{:S(2)}) copy-start(f32[128]{0:T(128)} %param.40) | copy-start | bytes 1540
  (6 other events, 11.7 us)
where the time goes:
time: 30.1 us; the launch traced here: 29.9 us
  Pallas kernels  15.3 us (51%)
  starting transfers between devices  11.2 us (37%)
  waiting for transfers between devices  1.24 us (4%)
  between operations  1.13 us (4%)
  local copies, waits for them, and re-layouts  0.95 us (3%)
    ppermute x6, starting transfers between devices, swapped(): return lax.ppermute(value, axis, pairs)  11.1 us
    pallas_call x1, Pallas kernels, body(): call(edge_kernel, [shape((n, latent), BF16), shape((edges, latent), BF16)...  6.47 us
    pallas_call x1, Pallas kernels, body(): call(functools.partial(pre_kernel, part=1), [shape((edges, latent), F32)]...  2.27 us
    pallas_call x1, Pallas kernels, body(): call(functools.partial(pre_kernel, part=2), [shape((edges, latent), F32)]...  2.23 us
    pallas_call x1, Pallas kernels, body(): call(target_kernel, [shape((n // 2, edges), BF16)], 10, in_specs=[VM, ANY])  1.57 us
    pallas_call x1, Pallas kernels, body(): call(own_kernel, [shape((edges, latent), F32)] + like(args[1], *args[3:])...  1.38 us
    ppermute x6, waiting for transfers between devices, swapped(): return lax.ppermute(value, axis, pairs)  1.24 us
    pallas_call x1, Pallas kernels, body(): call(fresh_kernel, [shape((n, latent), BF16)] + [shape((halo // 2, latent...  1.03 us
  transfers between devices with their start and end apart: 7, of which 2 were waited for; matrix products, arithmetic and copies ran while one was open for 0% of the time, Pallas kernels for 25%

commit v1 on v0

--- a/solution.py
+++ b/solution.py
@@ -68,6 +68,10 @@
     return jnp.concatenate(
         [jnp.concatenate([w, zero], axis=1), jnp.concatenate([zero, w], axis=1)], axis=0
     )
+
+
+def centred(w):
+    return w - jnp.mean(w, axis=-1, keepdims=True)
 
 
 def eight(row):
@@ -116,8 +120,8 @@
     lax.fori_loop(0, edge_ref.shape[0] // EDGE_BLOCK, step, 0)
 
 
-def target_kernel(recv_ref, _, marks_ref):
-    half = marks_ref.shape[0]
+def target_marks(recv_ref, marks_ref):
+    half = marks_ref.shape[1]
     one, zero = jnp.ones((), BF16), jnp.zeros((), BF16)
     ids = (lax.broadcasted_iota(jnp.int32, (half, LANES), 0) - half // 2).astype(F32).astype(BF16)
     recv = recv_ref[...]
@@ -126,23 +130,31 @@
     for b in range(recv.shape[0]):
         row = jnp.broadcast_to(low[b : b + 1, :], (16, LANES)).astype(BF16)
         row = jnp.concatenate([row] * (half // 16), axis=0)
-        marks_ref[:, b * LANES : (b + 1) * LANES] = jnp.where(ids == row, one, zero)
+        at = b % 2 * LANES
+        marks_ref[b // 2, :, at : at + LANES] = jnp.where(ids == row, one, zero)
+
+
+def window_kernel(
+    recv_ref, node_ref, mig_ref, _, marks_ref, old_ref, moved_ref,
+):
+    target_marks(recv_ref, marks_ref)
+    table = side_by_side(node_ref[...])
+    half_rows = table.shape[0]
+    n = 2 * half_rows
+    mig = mig_ref[...]
+    low, high = split_index(mig, half_rows)
+    moved = (mig - n).astype(F32).T.astype(BF16)
+    count = moved_ref.shape[1] // LANES
+    for b in range(n // LANES):
+        at = slice(b * LANES, (b + 1) * LANES)
+        old_ref[at, :] = lookup(low, high, b, table)
+        moved_ref[at, :] = marks_from(spread(moved, b), count, 0)
 
 
 def fresh_kernel(
-    node_ref, arrived_ref, recv_ref, halo_ref, cross_ref, fresh_ref, near_ref, far_ref, cross_out
+    old_ref, moved_ref, halo_ref, cross_ref, arrived_ref, fresh_ref, near_ref, far_ref, cross_out
 ):
-    table = side_by_side(node_ref[...])
-    n = 2 * table.shape[0]
-    recv = recv_ref[...]
-    low, high = split_index(recv, table.shape[0])
-    moved = (recv - n).astype(F32).T.astype(BF16)
-    arrived = arrived_ref[...]
-    pieces = []
-    for b in range(n // LANES):
-        marks = marks_from(spread(moved, b), arrived.shape[0] // LANES, 0)
-        pieces.append((lookup(low, high, b, table) + dot(marks, arrived)).astype(BF16))
-    fresh = jnp.concatenate(pieces, axis=0)
+    fresh = (old_ref[...] + dot(moved_ref[...], arrived_ref[...])).astype(BF16)
     fresh_ref[...] = fresh
     table = side_by_side(fresh)
     low, high = split_index(eight(halo_ref[...]), table.shape[0])
@@ -184,8 +196,7 @@
     remote_rows = jnp.concatenate([halo_ref[...], cross_ref[...]], axis=0)
     tx = dot(remote_rows, w1_ref[LANES : 2 * LANES, :]).astype(BF16)
     tx = jnp.concatenate([tx, jnp.zeros((2 * LANES - tx.shape[0], LANES), BF16)], axis=0)
-    w2 = w2_ref[...].astype(F32)
-    w2 = twice((w2 - jnp.mean(w2, axis=-1, keepdims=True)).astype(BF16))
+    w2 = twice(centred(w2_ref[...].astype(F32)).astype(BF16))
     gain, bias = gain_ref[...], bias_ref[...]
     acc_ref[...] = jnp.zeros_like(acc_ref)
 
@@ -214,7 +225,7 @@
 
     def gather_part(j, b):
         at = slice(2 * b * LANES, 2 * (b + 1) * LANES)
-        return dot(target_ref[:, rows_of(j, at.start, 2 * LANES)], packed_ref[at, :])
+        return dot(target_ref[j * quarters + b], packed_ref[at, :])
 
     def finish(j, b, centre, spreads, live, high):
         normed = centre * lax.rsqrt(spreads + EPSILON)
@@ -266,13 +277,12 @@
     for j in range(1, steps - 1):
         round_of(j, True, True)
     round_of(steps - 1, False, True)
-    acc_ref[...] += dot(target_ref[:, rows_of(steps - 1, 0, block)], packed_ref[...])
+    acc_ref[...] += sum(gather_part(steps - 1, b) for b in range(quarters))
 
     nb2 = nb2_ref[...]
     nb2 = nb2 - jnp.mean(nb2, axis=-1, keepdims=True)
     nb2 = jnp.concatenate([nb2, nb2], axis=1)
-    nw2 = nw2_ref[...].astype(F32)
-    nw2 = twice((nw2 - jnp.mean(nw2, axis=-1, keepdims=True)).astype(BF16))
+    nw2 = twice(centred(nw2_ref[...].astype(F32)).astype(BF16))
     nw1, nb1 = nw1_ref[...], nb1_ref[...]
     parts = 4
     size = nodes_half // parts
@@ -385,17 +395,23 @@
     )(*args, near)
     partner, own, recv = lax.optimization_barrier((partner, own, recv))
     outer, inner = outward(partner, far, d)
-    (targets,) = call(
-        target_kernel, [shape((n // 2, edges), BF16)], 10, in_specs=[VM, ANY]
-    )(recv, partner)
-    outer, inner, targets = lax.optimization_barrier((outer, inner, targets))
+    targets, *late = call(
+        window_kernel,
+        [
+            shape((edges // (2 * LANES), n // 2, 2 * LANES), BF16),
+            shape((n, latent), F32), shape((n, move), BF16),
+        ],
+        12,
+        in_specs=[VM] * 3 + [ANY],
+    )(recv, node_latent, mig, partner)
+    outer, inner, targets, *late = lax.optimization_barrier((outer, inner, targets, *late))
     arrived = inward(partner, outer, inner, d)
 
     fresh, near, far, cross_out = call(
         fresh_kernel,
         [shape((n, latent), BF16)] + [shape((halo // 2, latent), BF16)] * 2 + [shape((cross, latent), BF16)],
         8,
-    )(node_latent, arrived, mig, halo_index, cross_index)
+    )(*late, halo_index, cross_index, arrived)
     partner = swapped(near, "dom", lambda i: i ^ 1)
     cross_in = lax.ppermute(cross_out, "grp", [(i, i ^ 1) for i in range(lax.axis_size("grp"))])
     (pre,) = call(

time: 30.1 us -> 29.8 us (0.990)
  local copies, waits for them, and re-layouts: 0.95 us -> 1.9 us
  waiting for transfers between devices: 1.24 us -> 0.56 us
  Pallas kernels: 15.3 us -> 14.7 us
    unnamed x46, local copies, waits for them, and re-layouts: 0.94 us -> 1.89 us
    ppermute x6, waiting for transfers between devices: 1.24 us -> 0.55 us  [swapped(): return lax.ppermute(value, axis, pairs)]
    pallas_call x1, Pallas kernels: 1.03 us -> 0.61 us  [body(): call(fresh_kernel, [shape((n, latent), BF16)] + [shape((halo // 2, latent...]
where the time goes in v1:
time: 29.8 us; the launch traced here: 29.6 us
  Pallas kernels  14.7 us (49%)
  starting transfers between devices  11.2 us (38%)
  local copies, waits for them, and re-layouts  1.9 us (6%)
  between operations  1.12 us (4%)
  waiting for transfers between devices  0.56 us (2%)
    ppermute x6, starting transfers between devices, swapped(): return lax.ppermute(value, axis, pairs)  11.2 us
    pallas_call x1, Pallas kernels, body(): call(edge_kernel, [shape((n, latent), BF16), shape((edges, latent), BF16)...  6.34 us
    pallas_call x1, Pallas kernels, body(): call(functools.partial(pre_kernel, part=1), [shape((edges, latent), F32)]...  2.26 us
    pallas_call x1, Pallas kernels, body(): call(functools.partial(pre_kernel, part=2), [shape((edges, latent), F32)]...  2.23 us
    unnamed x46, local copies, waits for them, and re-layouts  1.89 us
    pallas_call x1, Pallas kernels, body(): call(window_kernel, [shape((edges // (2 * LANES), n // 2, 2 * LANES), BF1...  1.58 us
    pallas_call x1, Pallas kernels, body(): call(own_kernel, [shape((edges, latent), F32)] + like(args[1], *args[3:])...  1.38 us
    pallas_call x1, Pallas kernels, body(): call(fresh_kernel, [shape((n, latent), BF16)] + [shape((halo // 2, latent...  0.61 us
  transfers between devices with their start and end apart: 7, of which 2 were waited for; matrix products, arithmetic and copies ran while one was open for 0% of the time, Pallas kernels for 25%

profile of v1, /device:TPU:0, one launch (start us, length us, event | category | flops | bytes accessed | tf_op | source)
XLA Modules:
  0.0 29.6 jit_solution(2133563068119505797)
XLA Ops:
  0.6 0.0 copy-start.2
  0.7 0.0 copy-start
  0.8 0.8 %copy-done.2 = bf16[1024,128]{1,0:T(8,128)(2,1)S(1)} copy-done((bf16[1024,128]{1,0:T(8,128)(2,1)S(1)}, bf16[1024,128]{1,0:T(8,128)(2,1)}, u32[]{:S(2)}) %copy-start.2) | copy-done | bytes 262168
  1.6 0.3 %shard_map.213 = (bf16[128,128]{1,0:T(8,128)(2,1)S(1)}, bf16[128,128]{1,0:T(8,128)(2,1)S(1)}) custom-call(bf16[1024,128]{1,0:T(8,128)(2,1)S(1)} %copy-done.2, s32[1,256]{1,0:T(1,128)S(1)} %copy-done.12, f32[8,128]{1,0:T(8,128)S(1)} %shard_map.212._), custom_call_target="tpu_custom_call" | custom-call | flops 1000000000 | bytes 1000000 | tf_op jit(solution)/shard_map/pallas_call | solution.py:382
  1.9 3.0 %collective-permute-start = (bf16[128,128]{1,0:T(8,128)(2,1)S(1)}, bf16[128,128]{1,0:T(8,128)(2,1)S(1)}, u32[]{:S(2)}, u32[]{:S(2)}) collective-permute-start(bf16[128,128]{1,0:T(8,128)(2,1)S(1)} %get-tuple-element.34._), channel_id=1, source_target_pairs={{0,1},{1,0},{2,3},{3,2},{4,5},{5,4},{6,7},{7,6},{8,9},{9,8},{10,11... | collective-permute-start | bytes 98312 | tf_op jit(solution)/shard_map/ppermute | solution.py:29
  5.1 1.4 %shard_map.214 = (f32[6144,128]{1,0:T(8,128)S(1)}, bf16[384,128]{1,0:T(8,128)(2,1)S(1)}, s32[48,128]{1,0:T(8,128)S(1)}, s32[48,128]{1,0:T(8,128)S(1)}, s32[48,12...) custom-call(bf16[6144,128]{1,0:T(8,128)(2,1)S(1)} %copy-done, ...), custom_call_target="tpu_custom_call" | custom-call | flops 1000000000 | bytes 1000000 | tf_op jit(solution)/shard_map/pallas_call | solution.py:390
  6.5 0.4 %collective-permute-done._ = bf16[128,128]{1,0:T(8,128)(2,1)S(1)} collective-permute-done((bf16[128,128]{1,0:T(8,128)(2,1)S(1)}, bf16[128,128]{1,0:T(8,128)(2,1)S(1)}, u32[]{:S(2)}, u32[]{:S(2)}) %collective-permute-start) | collective-permute-done | bytes 32800 | tf_op jit(solution)/shard_map/ppermute | solution.py:29
  6.9 2.1 %collective-permute-start.2 = (bf16[128,128]{1,0:T(8,128)(2,1)S(1)}, bf16[128,128]{1,0:T(8,128)(2,1)S(1)}, u32[]{:S(2)}, u32[]{:S(2)}) collective-permute-start(bf16[128,128]{1,0:T(8,128)(2,1)S(1)} %get-tuple-element.66), channel_id=1, source_target_pairs={{0,2},{1,3},{2,0},{3,1},{4,6},{5,7},{6,4},{7,5},{8,10},{9,11},{10,... | collective-permute-start | bytes 98312 | tf_op jit(solution)/shard_map/ppermute | solution.py:29
  9.0 1.5 %collective-permute-start.1 = (bf16[128,128]{1,0:T(8,128)(2,1)S(1)}, bf16[128,128]{1,0:T(8,128)(2,1)S(1)}, u32[]{:S(2)}, u32[]{:S(2)}) collective-permute-start(bf16[128,128]{1,0:T(8,128)(2,1)S(1)} %get-tuple-element.67), channel_id=1, source_target_pairs={{0,1},{1,0},{2,4},{3,5},{4,2},{5,3},{6,8},{7,9},{8,6},{9,7},{10,12... | collective-permute-start | bytes 98312 | tf_op jit(solution)/shard_map/ppermute | solution.py:29
  10.5 0.9 %copy-done.3 = bf16[1024,128]{1,0:T(8,128)(2,1)S(1)} copy-done((bf16[1024,128]{1,0:T(8,128)(2,1)S(1)}, bf16[1024,128]{1,0:T(8,128)(2,1)}, u32[]{:S(2)}) %copy-start.3) | copy-done | bytes 262168
  11.4 1.6 %shard_map.215 = (bf16[24,512,256]{2,1,0:T(8,128)(2,1)S(1)}, f32[1024,128]{1,0:T(8,128)S(1)}, bf16[1024,256]{1,0:T(8,128)(2,1)S(1)}) custom-call(s32[48,128]{1,0:T(8,128)S(1)} %get-tuple-element.38.recv_ref.index_ref, bf16[1024,128]{1,0:T(8,128)(2,1)S(1)} %copy-done.3, s32[8,128]{1,0:T(8,128)S(1)} %get-tuple-element.39.mig_ref, ...), custom_call_target="tpu_custom_call" | custom-call | flops 1000000000 | bytes 1000000 | tf_op jit(solution)/shard_map/pallas_call | solution.py:398
  13.1 0.6 %shard_map.216 = (bf16[1024,128]{1,0:T(8,128)(2,1)S(1)}, bf16[64,128]{1,0:T(8,128)(2,1)S(1)}, bf16[64,128]{1,0:T(8,128)(2,1)S(1)}, bf16[32,128]{1,0:T(8,128)(2,1)S(1)}) custom-call(f32[1024,128]{1,0:T(8,128)S(1)} %get-tuple-element.43.old_ref, bf16[1024,256]{1,0:T(8,128)(2,1)S(1)} %get-tuple-element.44.moved_ref, s32[1,128]{1,0:T(1,128)S(1)} %get-tuple-element.45.halo_ref, ...), custom_call_target="tpu_custom_call" | custom-call | flops 1000000000 | bytes 1000000 | tf_op jit(solution)/shard_map/pallas_call | solution.py:410
  13.7 0.1 collective-permute-start.6
  13.8 1.4 %collective-permute-start.3 = (bf16[64,128]{1,0:T(8,128)(2,1)S(1)}, bf16[64,128]{1,0:T(8,128)(2,1)S(1)}, u32[]{:S(2)}, u32[]{:S(2)}) collective-permute-start(bf16[64,128]{1,0:T(8,128)(2,1)S(1)} %get-tuple-element.50._), channel_id=1, source_target_pairs={{0,1},{1,0},{2,3},{3,2},{4,5},{5,4},{6,7},{7,6},{8,9},{9,8},{10,11... | collective-permute-start | bytes 49160 | tf_op jit(solution)/shard_map/ppermute | solution.py:29
  15.2 2.2 %shard_map.217.before_ref = f32[6144,128]{1,0:T(8,128)S(1)} custom-call(f32[6144,128]{1,0:T(8,128)S(1)} %get-tuple-element.51.before_ref, bf16[1024,128]{1,0:T(8,128)(2,1)S(1)} %get-tuple-element.52.fresh_ref, s32[48,128]{1,0:T(8,128)S(1)} %get-tuple-element.38.recv_ref.index_ref, bf16[384,128]{1,0:T(8,128)(2,1)S(1)} %get-tuple-element.53.w_ref.w1_ref, ...), custom_call_target="tpu_custom_call" | custom-call | flops 1000000000 | bytes 1000000 | tf_op jit(solution)/shard_map/pallas_call | solution.py:417
  17.5 0.2 collective-permute-done.3._
  17.6 1.6 %collective-permute-start.5 = (bf16[64,128]{1,0:T(8,128)(2,1)S(1)}, bf16[64,128]{1,0:T(8,128)(2,1)S(1)}, u32[]{:S(2)}, u32[]{:S(2)}) collective-permute-start(bf16[64,128]{1,0:T(8,128)(2,1)S(1)} %get-tuple-element.70), channel_id=1, source_target_pairs={{0,2},{1,3},{2,0},{3,1},{4,6},{5,7},{6,4},{7,5},{8,10},{9,11},{10,... | collective-permute-start | bytes 49160 | tf_op jit(solution)/shard_map/ppermute | solution.py:29
  19.2 1.5 %collective-permute-start.4 = (bf16[64,128]{1,0:T(8,128)(2,1)S(1)}, bf16[64,128]{1,0:T(8,128)(2,1)S(1)}, u32[]{:S(2)}, u32[]{:S(2)}) collective-permute-start(bf16[64,128]{1,0:T(8,128)(2,1)S(1)} %get-tuple-element.71), channel_id=1, source_target_pairs={{0,1},{1,0},{2,4},{3,5},{4,2},{5,3},{6,8},{7,9},{8,6},{9,7},{10,12... | collective-permute-start | bytes 49160 | tf_op jit(solution)/shard_map/ppermute | solution.py:29
  20.7 0.0 copy-start.16
  20.8 0.0 copy-start.17
  20.8 0.0 copy-start.20
  20.8 0.0 copy-start.21
  20.8 2.3 %shard_map.218.pre_ref = f32[6144,128]{1,0:T(8,128)S(1)} custom-call(f32[6144,128]{1,0:T(8,128)S(1)} %shard_map.217.before_ref, bf16[1024,128]{1,0:T(8,128)(2,1)S(1)} %get-tuple-element.52.fresh_ref, s32[48,128]{1,0:T(8,128)S(1)} %get-tuple-element.57.index_ref.send_ref, bf16[384,128]{1,0:T(8,128)(2,1)S(1)} %get-tuple-element.53.w_ref.w1_ref, ...), custom_call_target="tpu_custom_call" | custom-call | flops 1000000000 | bytes 1000000 | tf_op jit(solution)/shard_map/pallas_call | solution.py:423
  23.3 6.3 %shard_map.219 = (bf16[1024,128]{1,0:T(8,128)(2,1)}, bf16[6144,128]{1,0:T(8,128)(2,1)}) custom-call(f32[6144,128]{1,0:T(8,128)S(1)} %shard_map.218.pre_ref, bf16[6144,128]{1,0:T(8,128)(2,1)S(1)} %copy-done.1, bf16[1024,128]{1,0:T(8,128)(2,1)S(1)} %get-tuple-element.52.fresh_ref, bf16[128,128]{1,0:T(8,128)(2,1)S(1)} %pad_maximum_fusion.3.halo_ref, ...), custom_call_target="tpu_custom_call" | custom-call | flops 10000000000 | bytes 1000000 | tf_op jit(solution)/shard_map/pallas_call | solution.py:429
  (56 shorter events, 0.2 us)
Async XLA Ops:
  0.7 4.3 %copy-start = (bf16[6144,128]{1,0:T(8,128)(2,1)S(1)}, bf16[6144,128]{1,0:T(8,128)(2,1)}, u32[]{:S(2)}) copy-start(bf16[6144,128]{1,0:T(8,128)(2,1)} %edge_ref.3) | copy-start | bytes 4718596
  0.7 4.3 %copy-start.13 = (f32[128]{0:T(128)S(1)}, f32[128]{0:T(128)}, u32[]{:S(2)}) copy-start(f32[128]{0:T(128)} %param.31) | copy-start | bytes 1540
  0.7 4.3 %copy-start.4 = (bf16[384,128]{1,0:T(8,128)(2,1)S(1)}, bf16[384,128]{1,0:T(8,128)(2,1)}, u32[]{:S(2)}) copy-start(bf16[384,128]{1,0:T(8,128)(2,1)} %w1_ref.1) | copy-start | bytes 294916
  0.7 4.3 %copy-start.10 = (s32[6144]{0:T(1024)S(1)}, s32[6144]{0:T(1024)}, u32[]{:S(2)}) copy-start(s32[6144]{0:T(1024)} %param.29) | copy-start | bytes 73732
  0.7 4.3 %copy-start.9 = (s32[6144]{0:T(1024)S(1)}, s32[6144]{0:T(1024)}, u32[]{:S(2)}) copy-start(s32[6144]{0:T(1024)} %param.28) | copy-start | bytes 73732
  0.7 4.3 %copy-start.8 = (s32[6144]{0:T(1024)S(1)}, s32[6144]{0:T(1024)}, u32[]{:S(2)}) copy-start(s32[6144]{0:T(1024)} %param.27) | copy-start | bytes 73732
  0.7 4.3 %copy-start.15 = (s32[1,32]{1,0:T(1,128)S(1)}, s32[1,32]{1,0:T(1,128)}, u32[]{:S(2)}) copy-start(s32[1,32]{1,0:T(1,128)} %cross_ref.1) | copy-start | bytes 388
  0.7 4.3 %copy-start.14 = (s32[1,128]{1,0:T(1,128)S(1)}, s32[1,128]{1,0:T(1,128)}, u32[]{:S(2)}) copy-start(s32[1,128]{1,0:T(1,128)} %halo_ref.1) | copy-start | bytes 1540
  0.7 4.3 %copy-start.11 = (s32[1024]{0:T(1024)S(1)}, s32[1024]{0:T(1024)}, u32[]{:S(2)}) copy-start(s32[1024]{0:T(1024)} %param.24) | copy-start | bytes 12292
  1.9 4.9 %collective-permute-start = (bf16[128,128]{1,0:T(8,128)(2,1)S(1)}, bf16[128,128]{1,0:T(8,128)(2,1)S(1)}, u32[]{:S(2)}, u32[]{:S(2)}) collective-permute-start(bf16[128,128]{1,0:T(8,128)(2,1)S(1)} %get-tuple-element.34._), channel_id=1, source_target_pairs={{0,1},{1,0},{2,3},{3,2},{4,5},{5,4},{6,7},{7,6},{8,9},{9,8},{10,11... | collective-permute-start | bytes 98312 | tf_op jit(solution)/shard_map/ppermute | solution.py:29
  6.9 6.1 %collective-permute-start.2 = (bf16[128,128]{1,0:T(8,128)(2,1)S(1)}, bf16[128,128]{1,0:T(8,128)(2,1)S(1)}, u32[]{:S(2)}, u32[]{:S(2)}) collective-permute-start(bf16[128,128]{1,0:T(8,128)(2,1)S(1)} %get-tuple-element.66), channel_id=1, source_target_pairs={{0,2},{1,3},{2,0},{3,1},{4,6},{5,7},{6,4},{7,5},{8,10},{9,11},{10,... | collective-permute-start | bytes 98312 | tf_op jit(solution)/shard_map/ppermute | solution.py:29
  9.0 4.0 %collective-permute-start.1 = (bf16[128,128]{1,0:T(8,128)(2,1)S(1)}, bf16[128,128]{1,0:T(8,128)(2,1)S(1)}, u32[]{:S(2)}, u32[]{:S(2)}) collective-permute-start(bf16[128,128]{1,0:T(8,128)(2,1)S(1)} %get-tuple-element.67), channel_id=1, source_target_pairs={{0,1},{1,0},{2,4},{3,5},{4,2},{5,3},{6,8},{7,9},{8,6},{9,7},{10,12... | collective-permute-start | bytes 98312 | tf_op jit(solution)/shard_map/ppermute | solution.py:29
  13.7 9.4 %collective-permute-start.6 = (bf16[32,128]{1,0:T(8,128)(2,1)S(1)}, bf16[32,128]{1,0:T(8,128)(2,1)S(1)}, u32[]{:S(2)}, u32[]{:S(2)}) collective-permute-start(bf16[32,128]{1,0:T(8,128)(2,1)S(1)} %get-tuple-element.55), channel_id=1, source_target_pairs={{0,16},{16,0},{1,17},{17,1},{2,18},{18,2},{3,19},{19,3},{4,20},{20... | collective-permute-start | bytes 24584 | tf_op jit(solution)/shard_map/ppermute | solution.py:416
  13.8 3.8 %collective-permute-start.3 = (bf16[64,128]{1,0:T(8,128)(2,1)S(1)}, bf16[64,128]{1,0:T(8,128)(2,1)S(1)}, u32[]{:S(2)}, u32[]{:S(2)}) collective-permute-start(bf16[64,128]{1,0:T(8,128)(2,1)S(1)} %get-tuple-element.50._), channel_id=1, source_target_pairs={{0,1},{1,0},{2,3},{3,2},{4,5},{5,4},{6,7},{7,6},{8,9},{9,8},{10,11... | collective-permute-start | bytes 49160 | tf_op jit(solution)/shard_map/ppermute | solution.py:29
  17.6 5.5 %collective-permute-start.5 = (bf16[64,128]{1,0:T(8,128)(2,1)S(1)}, bf16[64,128]{1,0:T(8,128)(2,1)S(1)}, u32[]{:S(2)}, u32[]{:S(2)}) collective-permute-start(bf16[64,128]{1,0:T(8,128)(2,1)S(1)} %get-tuple-element.70), channel_id=1, source_target_pairs={{0,2},{1,3},{2,0},{3,1},{4,6},{5,7},{6,4},{7,5},{8,10},{9,11},{10,... | collective-permute-start | bytes 49160 | tf_op jit(solution)/shard_map/ppermute | solution.py:29
  19.2 3.9 %collective-permute-start.4 = (bf16[64,128]{1,0:T(8,128)(2,1)S(1)}, bf16[64,128]{1,0:T(8,128)(2,1)S(1)}, u32[]{:S(2)}, u32[]{:S(2)}) collective-permute-start(bf16[64,128]{1,0:T(8,128)(2,1)S(1)} %get-tuple-element.71), channel_id=1, source_target_pairs={{0,1},{1,0},{2,4},{3,5},{4,2},{5,3},{6,8},{7,9},{8,6},{9,7},{10,12... | collective-permute-start | bytes 49160 | tf_op jit(solution)/shard_map/ppermute | solution.py:29
  20.7 2.5 %copy-start.7 = (bf16[128,128]{1,0:T(8,128)(2,1)S(1)}, bf16[128,128]{1,0:T(8,128)(2,1)}, u32[]{:S(2)}) copy-start(bf16[128,128]{1,0:T(8,128)(2,1)} %nw2_ref.1) | copy-start | bytes 98308
  20.7 2.5 %copy-start.16 = (f32[128]{0:T(128)S(1)}, f32[128]{0:T(128)}, u32[]{:S(2)}) copy-start(f32[128]{0:T(128)} %param.33) | copy-start | bytes 1540
  20.8 2.5 %copy-start.17 = (f32[128]{0:T(128)S(1)}, f32[128]{0:T(128)}, u32[]{:S(2)}) copy-start(f32[128]{0:T(128)} %param.34) | copy-start | bytes 1540
  20.8 2.5 %copy-start.18 = (f32[128]{0:T(128)S(1)}, f32[128]{0:T(128)}, u32[]{:S(2)}) copy-start(f32[128]{0:T(128)} %param.35) | copy-start | bytes 1540
  20.8 2.5 %copy-start.19 = (f32[128]{0:T(128)S(1)}, f32[128]{0:T(128)}, u32[]{:S(2)}) copy-start(f32[128]{0:T(128)} %param.37) | copy-start | bytes 1540
  20.8 2.5 %copy-start.20 = (f32[128]{0:T(128)S(1)}, f32[128]{0:T(128)}, u32[]{:S(2)}) copy-start(f32[128]{0:T(128)} %param.39) | copy-start | bytes 1540
  20.8 2.5 %copy-start.21 = (f32[128]{0:T(128)S(1)}, f32[128]{0:T(128)}, u32[]{:S(2)}) copy-start(f32[128]{0:T(128)} %param.40) | copy-start | bytes 1540
  20.8 2.5 %copy-start.22 = (f32[128]{0:T(128)S(1)}, f32[128]{0:T(128)}, u32[]{:S(2)}) copy-start(f32[128]{0:T(128)} %param.41) | copy-start | bytes 1540
  (6 other events, 10.2 us)

commit v2 on v1

--- a/solution.py
+++ b/solution.py
@@ -147,14 +147,14 @@
     count = moved_ref.shape[1] // LANES
     for b in range(n // LANES):
         at = slice(b * LANES, (b + 1) * LANES)
-        old_ref[at, :] = lookup(low, high, b, table)
+        old_ref[at, :] = lookup(low, high, b, table).astype(BF16)
         moved_ref[at, :] = marks_from(spread(moved, b), count, 0)
 
 
 def fresh_kernel(
     old_ref, moved_ref, halo_ref, cross_ref, arrived_ref, fresh_ref, near_ref, far_ref, cross_out
 ):
-    fresh = (old_ref[...] + dot(moved_ref[...], arrived_ref[...])).astype(BF16)
+    fresh = (old_ref[...].astype(F32) + dot(moved_ref[...], arrived_ref[...])).astype(BF16)
     fresh_ref[...] = fresh
     table = side_by_side(fresh)
     low, high = split_index(eight(halo_ref[...]), table.shape[0])
@@ -399,7 +399,7 @@
         window_kernel,
         [
             shape((edges // (2 * LANES), n // 2, 2 * LANES), BF16),
-            shape((n, latent), F32), shape((n, move), BF16),
+            shape((n, latent), BF16), shape((n, move), BF16),
         ],
         12,
         in_specs=[VM] * 3 + [ANY],

time: 29.8 us -> 29.8 us (level)
  no operation moved by 1% of the time
where the time goes in v2:
time: 29.8 us; the launch traced here: 29.6 us
  Pallas kernels  14.7 us (49%)
  starting transfers between devices  11.2 us (38%)
  local copies, waits for them, and re-layouts  1.9 us (6%)
  between operations  1.12 us (4%)
  waiting for transfers between devices  0.56 us (2%)
    ppermute x6, starting transfers between devices, swapped(): return lax.ppermute(value, axis, pairs)  11.2 us
    pallas_call x1, Pallas kernels, body(): call(edge_kernel, [shape((n, latent), BF16), shape((edges, latent), BF16)...  6.33 us
    pallas_call x1, Pallas kernels, body(): call(functools.partial(pre_kernel, part=1), [shape((edges, latent), F32)]...  2.27 us
    pallas_call x1, Pallas kernels, body(): call(functools.partial(pre_kernel, part=2), [shape((edges, latent), F32)]...  2.23 us
    unnamed x46, local copies, waits for them, and re-layouts  1.89 us
    pallas_call x1, Pallas kernels, body(): call(window_kernel, [shape((edges // (2 * LANES), n // 2, 2 * LANES), BF1...  1.58 us
    pallas_call x1, Pallas kernels, body(): call(own_kernel, [shape((edges, latent), F32)] + like(args[1], *args[3:])...  1.38 us
    pallas_call x1, Pallas kernels, body(): call(fresh_kernel, [shape((n, latent), BF16)] + [shape((halo // 2, latent...  0.61 us
  transfers between devices with their start and end apart: 7, of which 2 were waited for; matrix products, arithmetic and copies ran while one was open for 0% of the time, Pallas kernels for 25%

profile of v2, /device:TPU:0, one launch (start us, length us, event | category | flops | bytes accessed | tf_op | source)
XLA Modules:
  0.0 29.6 jit_solution(5559754256566323669)
XLA Ops:
  0.6 0.0 copy-start.2
  0.7 0.0 copy-start
  0.8 0.8 %copy-done.2 = bf16[1024,128]{1,0:T(8,128)(2,1)S(1)} copy-done((bf16[1024,128]{1,0:T(8,128)(2,1)S(1)}, bf16[1024,128]{1,0:T(8,128)(2,1)}, u32[]{:S(2)}) %copy-start.2) | copy-done | bytes 262168
  1.6 0.3 %shard_map.213 = (bf16[128,128]{1,0:T(8,128)(2,1)S(1)}, bf16[128,128]{1,0:T(8,128)(2,1)S(1)}) custom-call(bf16[1024,128]{1,0:T(8,128)(2,1)S(1)} %copy-done.2, s32[1,256]{1,0:T(1,128)S(1)} %copy-done.12, f32[8,128]{1,0:T(8,128)S(1)} %shard_map.212._), custom_call_target="tpu_custom_call" | custom-call | flops 1000000000 | bytes 1000000 | tf_op jit(solution)/shard_map/pallas_call | solution.py:382
  1.9 3.0 %collective-permute-start = (bf16[128,128]{1,0:T(8,128)(2,1)S(1)}, bf16[128,128]{1,0:T(8,128)(2,1)S(1)}, u32[]{:S(2)}, u32[]{:S(2)}) collective-permute-start(bf16[128,128]{1,0:T(8,128)(2,1)S(1)} %get-tuple-element.34._), channel_id=1, source_target_pairs={{0,1},{1,0},{2,3},{3,2},{4,5},{5,4},{6,7},{7,6},{8,9},{9,8},{10,11... | collective-permute-start | bytes 98312 | tf_op jit(solution)/shard_map/ppermute | solution.py:29
  5.1 1.4 %shard_map.214 = (f32[6144,128]{1,0:T(8,128)S(1)}, bf16[384,128]{1,0:T(8,128)(2,1)S(1)}, s32[48,128]{1,0:T(8,128)S(1)}, s32[48,128]{1,0:T(8,128)S(1)}, s32[48,12...) custom-call(bf16[6144,128]{1,0:T(8,128)(2,1)S(1)} %copy-done, ...), custom_call_target="tpu_custom_call" | custom-call | flops 1000000000 | bytes 1000000 | tf_op jit(solution)/shard_map/pallas_call | solution.py:390
  6.5 0.4 %collective-permute-done._ = bf16[128,128]{1,0:T(8,128)(2,1)S(1)} collective-permute-done((bf16[128,128]{1,0:T(8,128)(2,1)S(1)}, bf16[128,128]{1,0:T(8,128)(2,1)S(1)}, u32[]{:S(2)}, u32[]{:S(2)}) %collective-permute-start) | collective-permute-done | bytes 32800 | tf_op jit(solution)/shard_map/ppermute | solution.py:29
  6.9 2.1 %collective-permute-start.2 = (bf16[128,128]{1,0:T(8,128)(2,1)S(1)}, bf16[128,128]{1,0:T(8,128)(2,1)S(1)}, u32[]{:S(2)}, u32[]{:S(2)}) collective-permute-start(bf16[128,128]{1,0:T(8,128)(2,1)S(1)} %get-tuple-element.66), channel_id=1, source_target_pairs={{0,2},{1,3},{2,0},{3,1},{4,6},{5,7},{6,4},{7,5},{8,10},{9,11},{10,... | collective-permute-start | bytes 98312 | tf_op jit(solution)/shard_map/ppermute | solution.py:29
  9.0 1.5 %collective-permute-start.1 = (bf16[128,128]{1,0:T(8,128)(2,1)S(1)}, bf16[128,128]{1,0:T(8,128)(2,1)S(1)}, u32[]{:S(2)}, u32[]{:S(2)}) collective-permute-start(bf16[128,128]{1,0:T(8,128)(2,1)S(1)} %get-tuple-element.67), channel_id=1, source_target_pairs={{0,1},{1,0},{2,4},{3,5},{4,2},{5,3},{6,8},{7,9},{8,6},{9,7},{10,12... | collective-permute-start | bytes 98312 | tf_op jit(solution)/shard_map/ppermute | solution.py:29
  10.5 0.9 %copy-done.3 = bf16[1024,128]{1,0:T(8,128)(2,1)S(1)} copy-done((bf16[1024,128]{1,0:T(8,128)(2,1)S(1)}, bf16[1024,128]{1,0:T(8,128)(2,1)}, u32[]{:S(2)}) %copy-start.3) | copy-done | bytes 262168
  11.4 1.6 %shard_map.215 = (bf16[24,512,256]{2,1,0:T(8,128)(2,1)S(1)}, bf16[1024,128]{1,0:T(8,128)(2,1)S(1)}, bf16[1024,256]{1,0:T(8,128)(2,1)S(1)}) custom-call(s32[48,128]{1,0:T(8,128)S(1)} %get-tuple-element.38.recv_ref.index_ref, bf16[1024,128]{1,0:T(8,128)(2,1)S(1)} %copy-done.3, s32[8,128]{1,0:T(8,128)S(1)} %get-tuple-element.39.mig_ref, ...), custom_call_target="tpu_custom_call" | custom-call | flops 1000000000 | bytes 1000000 | tf_op jit(solution)/shard_map/pallas_call | solution.py:398
  13.1 0.6 %shard_map.216 = (bf16[1024,128]{1,0:T(8,128)(2,1)S(1)}, bf16[64,128]{1,0:T(8,128)(2,1)S(1)}, bf16[64,128]{1,0:T(8,128)(2,1)S(1)}, bf16[32,128]{1,0:T(8,128)(2,1)S(1)}) custom-call(bf16[1024,128]{1,0:T(8,128)(2,1)S(1)} %get-tuple-element.43.old_ref, bf16[1024,256]{1,0:T(8,128)(2,1)S(1)} %get-tuple-element.44.moved_ref, ...), custom_call_target="tpu_custom_call" | custom-call | flops 1000000000 | bytes 1000000 | tf_op jit(solution)/shard_map/pallas_call | solution.py:410
  13.7 0.1 collective-permute-start.6
  13.8 1.4 %collective-permute-start.3 = (bf16[64,128]{1,0:T(8,128)(2,1)S(1)}, bf16[64,128]{1,0:T(8,128)(2,1)S(1)}, u32[]{:S(2)}, u32[]{:S(2)}) collective-permute-start(bf16[64,128]{1,0:T(8,128)(2,1)S(1)} %get-tuple-element.50._), channel_id=1, source_target_pairs={{0,1},{1,0},{2,3},{3,2},{4,5},{5,4},{6,7},{7,6},{8,9},{9,8},{10,11... | collective-permute-start | bytes 49160 | tf_op jit(solution)/shard_map/ppermute | solution.py:29
  15.2 2.2 %shard_map.217.before_ref = f32[6144,128]{1,0:T(8,128)S(1)} custom-call(f32[6144,128]{1,0:T(8,128)S(1)} %get-tuple-element.51.before_ref, bf16[1024,128]{1,0:T(8,128)(2,1)S(1)} %get-tuple-element.52.fresh_ref, s32[48,128]{1,0:T(8,128)S(1)} %get-tuple-element.38.recv_ref.index_ref, bf16[384,128]{1,0:T(8,128)(2,1)S(1)} %get-tuple-element.53.w_ref.w1_ref, ...), custom_call_target="tpu_custom_call" | custom-call | flops 1000000000 | bytes 1000000 | tf_op jit(solution)/shard_map/pallas_call | solution.py:417
  17.5 0.2 collective-permute-done.3._
  17.6 1.6 %collective-permute-start.5 = (bf16[64,128]{1,0:T(8,128)(2,1)S(1)}, bf16[64,128]{1,0:T(8,128)(2,1)S(1)}, u32[]{:S(2)}, u32[]{:S(2)}) collective-permute-start(bf16[64,128]{1,0:T(8,128)(2,1)S(1)} %get-tuple-element.70), channel_id=1, source_target_pairs={{0,2},{1,3},{2,0},{3,1},{4,6},{5,7},{6,4},{7,5},{8,10},{9,11},{10,... | collective-permute-start | bytes 49160 | tf_op jit(solution)/shard_map/ppermute | solution.py:29
  19.3 1.5 %collective-permute-start.4 = (bf16[64,128]{1,0:T(8,128)(2,1)S(1)}, bf16[64,128]{1,0:T(8,128)(2,1)S(1)}, u32[]{:S(2)}, u32[]{:S(2)}) collective-permute-start(bf16[64,128]{1,0:T(8,128)(2,1)S(1)} %get-tuple-element.71), channel_id=1, source_target_pairs={{0,1},{1,0},{2,4},{3,5},{4,2},{5,3},{6,8},{7,9},{8,6},{9,7},{10,12... | collective-permute-start | bytes 49160 | tf_op jit(solution)/shard_map/ppermute | solution.py:29
  20.7 0.0 copy-start.16
  20.8 0.0 copy-start.18
  20.8 0.0 copy-start.19
  20.8 0.0 copy-start.22
  20.8 2.3 %shard_map.218.pre_ref = f32[6144,128]{1,0:T(8,128)S(1)} custom-call(f32[6144,128]{1,0:T(8,128)S(1)} %shard_map.217.before_ref, bf16[1024,128]{1,0:T(8,128)(2,1)S(1)} %get-tuple-element.52.fresh_ref, s32[48,128]{1,0:T(8,128)S(1)} %get-tuple-element.57.index_ref.send_ref, bf16[384,128]{1,0:T(8,128)(2,1)S(1)} %get-tuple-element.53.w_ref.w1_ref, ...), custom_call_target="tpu_custom_call" | custom-call | flops 1000000000 | bytes 1000000 | tf_op jit(solution)/shard_map/pallas_call | solution.py:423
  23.3 6.3 %shard_map.219 = (bf16[1024,128]{1,0:T(8,128)(2,1)}, bf16[6144,128]{1,0:T(8,128)(2,1)}) custom-call(f32[6144,128]{1,0:T(8,128)S(1)} %shard_map.218.pre_ref, bf16[6144,128]{1,0:T(8,128)(2,1)S(1)} %copy-done.1, bf16[1024,128]{1,0:T(8,128)(2,1)S(1)} %get-tuple-element.52.fresh_ref, bf16[128,128]{1,0:T(8,128)(2,1)S(1)} %pad_maximum_fusion.3.halo_ref, ...), custom_call_target="tpu_custom_call" | custom-call | flops 10000000000 | bytes 1000000 | tf_op jit(solution)/shard_map/pallas_call | solution.py:429
  (56 shorter events, 0.2 us)
Async XLA Ops:
  0.7 4.3 %copy-start = (bf16[6144,128]{1,0:T(8,128)(2,1)S(1)}, bf16[6144,128]{1,0:T(8,128)(2,1)}, u32[]{:S(2)}) copy-start(bf16[6144,128]{1,0:T(8,128)(2,1)} %edge_ref.3) | copy-start | bytes 4718596
  0.7 4.3 %copy-start.13 = (f32[128]{0:T(128)S(1)}, f32[128]{0:T(128)}, u32[]{:S(2)}) copy-start(f32[128]{0:T(128)} %param.31) | copy-start | bytes 1540
  0.7 4.3 %copy-start.4 = (bf16[384,128]{1,0:T(8,128)(2,1)S(1)}, bf16[384,128]{1,0:T(8,128)(2,1)}, u32[]{:S(2)}) copy-start(bf16[384,128]{1,0:T(8,128)(2,1)} %w1_ref.1) | copy-start | bytes 294916
  0.7 4.3 %copy-start.10 = (s32[6144]{0:T(1024)S(1)}, s32[6144]{0:T(1024)}, u32[]{:S(2)}) copy-start(s32[6144]{0:T(1024)} %param.29) | copy-start | bytes 73732
  0.7 4.3 %copy-start.9 = (s32[6144]{0:T(1024)S(1)}, s32[6144]{0:T(1024)}, u32[]{:S(2)}) copy-start(s32[6144]{0:T(1024)} %param.28) | copy-start | bytes 73732
  0.7 4.3 %copy-start.8 = (s32[6144]{0:T(1024)S(1)}, s32[6144]{0:T(1024)}, u32[]{:S(2)}) copy-start(s32[6144]{0:T(1024)} %param.27) | copy-start | bytes 73732
  0.7 4.3 %copy-start.15 = (s32[1,32]{1,0:T(1,128)S(1)}, s32[1,32]{1,0:T(1,128)}, u32[]{:S(2)}) copy-start(s32[1,32]{1,0:T(1,128)} %cross_ref.1) | copy-start | bytes 388
  0.7 4.3 %copy-start.14 = (s32[1,128]{1,0:T(1,128)S(1)}, s32[1,128]{1,0:T(1,128)}, u32[]{:S(2)}) copy-start(s32[1,128]{1,0:T(1,128)} %halo_ref.1) | copy-start | bytes 1540
  0.7 4.3 %copy-start.11 = (s32[1024]{0:T(1024)S(1)}, s32[1024]{0:T(1024)}, u32[]{:S(2)}) copy-start(s32[1024]{0:T(1024)} %param.24) | copy-start | bytes 12292
  1.9 4.9 %collective-permute-start = (bf16[128,128]{1,0:T(8,128)(2,1)S(1)}, bf16[128,128]{1,0:T(8,128)(2,1)S(1)}, u32[]{:S(2)}, u32[]{:S(2)}) collective-permute-start(bf16[128,128]{1,0:T(8,128)(2,1)S(1)} %get-tuple-element.34._), channel_id=1, source_target_pairs={{0,1},{1,0},{2,3},{3,2},{4,5},{5,4},{6,7},{7,6},{8,9},{9,8},{10,11... | collective-permute-start | bytes 98312 | tf_op jit(solution)/shard_map/ppermute | solution.py:29
  6.9 6.1 %collective-permute-start.2 = (bf16[128,128]{1,0:T(8,128)(2,1)S(1)}, bf16[128,128]{1,0:T(8,128)(2,1)S(1)}, u32[]{:S(2)}, u32[]{:S(2)}) collective-permute-start(bf16[128,128]{1,0:T(8,128)(2,1)S(1)} %get-tuple-element.66), channel_id=1, source_target_pairs={{0,2},{1,3},{2,0},{3,1},{4,6},{5,7},{6,4},{7,5},{8,10},{9,11},{10,... | collective-permute-start | bytes 98312 | tf_op jit(solution)/shard_map/ppermute | solution.py:29
  9.0 4.0 %collective-permute-start.1 = (bf16[128,128]{1,0:T(8,128)(2,1)S(1)}, bf16[128,128]{1,0:T(8,128)(2,1)S(1)}, u32[]{:S(2)}, u32[]{:S(2)}) collective-permute-start(bf16[128,128]{1,0:T(8,128)(2,1)S(1)} %get-tuple-element.67), channel_id=1, source_target_pairs={{0,1},{1,0},{2,4},{3,5},{4,2},{5,3},{6,8},{7,9},{8,6},{9,7},{10,12... | collective-permute-start | bytes 98312 | tf_op jit(solution)/shard_map/ppermute | solution.py:29
  13.7 9.4 %collective-permute-start.6 = (bf16[32,128]{1,0:T(8,128)(2,1)S(1)}, bf16[32,128]{1,0:T(8,128)(2,1)S(1)}, u32[]{:S(2)}, u32[]{:S(2)}) collective-permute-start(bf16[32,128]{1,0:T(8,128)(2,1)S(1)} %get-tuple-element.55), channel_id=1, source_target_pairs={{0,16},{16,0},{1,17},{17,1},{2,18},{18,2},{3,19},{19,3},{4,20},{20... | collective-permute-start | bytes 24584 | tf_op jit(solution)/shard_map/ppermute | solution.py:416
  13.8 3.8 %collective-permute-start.3 = (bf16[64,128]{1,0:T(8,128)(2,1)S(1)}, bf16[64,128]{1,0:T(8,128)(2,1)S(1)}, u32[]{:S(2)}, u32[]{:S(2)}) collective-permute-start(bf16[64,128]{1,0:T(8,128)(2,1)S(1)} %get-tuple-element.50._), channel_id=1, source_target_pairs={{0,1},{1,0},{2,3},{3,2},{4,5},{5,4},{6,7},{7,6},{8,9},{9,8},{10,11... | collective-permute-start | bytes 49160 | tf_op jit(solution)/shard_map/ppermute | solution.py:29
  17.6 5.5 %collective-permute-start.5 = (bf16[64,128]{1,0:T(8,128)(2,1)S(1)}, bf16[64,128]{1,0:T(8,128)(2,1)S(1)}, u32[]{:S(2)}, u32[]{:S(2)}) collective-permute-start(bf16[64,128]{1,0:T(8,128)(2,1)S(1)} %get-tuple-element.70), channel_id=1, source_target_pairs={{0,2},{1,3},{2,0},{3,1},{4,6},{5,7},{6,4},{7,5},{8,10},{9,11},{10,... | collective-permute-start | bytes 49160 | tf_op jit(solution)/shard_map/ppermute | solution.py:29
  19.3 3.9 %collective-permute-start.4 = (bf16[64,128]{1,0:T(8,128)(2,1)S(1)}, bf16[64,128]{1,0:T(8,128)(2,1)S(1)}, u32[]{:S(2)}, u32[]{:S(2)}) collective-permute-start(bf16[64,128]{1,0:T(8,128)(2,1)S(1)} %get-tuple-element.71), channel_id=1, source_target_pairs={{0,1},{1,0},{2,4},{3,5},{4,2},{5,3},{6,8},{7,9},{8,6},{9,7},{10,12... | collective-permute-start | bytes 49160 | tf_op jit(solution)/shard_map/ppermute | solution.py:29
  20.7 2.5 %copy-start.7 = (bf16[128,128]{1,0:T(8,128)(2,1)S(1)}, bf16[128,128]{1,0:T(8,128)(2,1)}, u32[]{:S(2)}) copy-start(bf16[128,128]{1,0:T(8,128)(2,1)} %nw2_ref.1) | copy-start | bytes 98308
  20.7 2.5 %copy-start.16 = (f32[128]{0:T(128)S(1)}, f32[128]{0:T(128)}, u32[]{:S(2)}) copy-start(f32[128]{0:T(128)} %param.33) | copy-start | bytes 1540
  20.8 2.5 %copy-start.17 = (f32[128]{0:T(128)S(1)}, f32[128]{0:T(128)}, u32[]{:S(2)}) copy-start(f32[128]{0:T(128)} %param.34) | copy-start | bytes 1540
  20.8 2.5 %copy-start.18 = (f32[128]{0:T(128)S(1)}, f32[128]{0:T(128)}, u32[]{:S(2)}) copy-start(f32[128]{0:T(128)} %param.35) | copy-start | bytes 1540
  20.8 2.5 %copy-start.19 = (f32[128]{0:T(128)S(1)}, f32[128]{0:T(128)}, u32[]{:S(2)}) copy-start(f32[128]{0:T(128)} %param.37) | copy-start | bytes 1540
  20.8 2.5 %copy-start.20 = (f32[128]{0:T(128)S(1)}, f32[128]{0:T(128)}, u32[]{:S(2)}) copy-start(f32[128]{0:T(128)} %param.39) | copy-start | bytes 1540
  20.8 2.5 %copy-start.21 = (f32[128]{0:T(128)S(1)}, f32[128]{0:T(128)}, u32[]{:S(2)}) copy-start(f32[128]{0:T(128)} %param.40) | copy-start | bytes 1540
  20.8 2.5 %copy-start.22 = (f32[128]{0:T(128)S(1)}, f32[128]{0:T(128)}, u32[]{:S(2)}) copy-start(f32[128]{0:T(128)} %param.41) | copy-start | bytes 1540
  (6 other events, 10.2 us)
